TPU v7x, 256 devices: a whole 4x4x8 slice. The times are simulated.
256 devices in a mesh: dp: 32 (over y_hi, z, core), vocab: 8 (over x, y_lo).
Axes of the slice: x: 4, y: 4 (y_hi: 2, y_lo: 2; y = y_hi * 2 + y_lo), z: 8, core: 2. Of those that a mesh axis runs over, the one named last changes fastest.
Arguments:
- hidden: bfloat16 [16384, 3072], P(('dp', 'vocab')), may hold values from -128 to 128
- targets: int32 [16384], P(('dp', 'vocab')), may hold values from 0 to 16383
- lengths: int32 [32], P('dp'), may hold values from 1 to 512
- head: bfloat16 [3072, 16384], P('dp', 'vocab'), may hold values from -1 to 1
Outputs:
- grad_hidden: bfloat16 [16384, 3072], P(('dp', 'vocab'))
- loss: float32 [], replicated
All inputs are finite; a program needn't handle non-finite values.
Results may differ from a plain program's by a relative error of at most 0.0052.
Values may be sent and summed in bfloat16 or wider, within the bound.
A program may use at most 64 MiB of HBM per device.

v0:
```python
import functools
import jax
import jax.numpy as jnp
from jax import lax
from jax.sharding import Mesh
from jax.sharding import PartitionSpec as P

DP = ("dp_0", "dp_1", "dp_2")
VOCAB = ("vocab_0", "vocab_1")
DP_VOCAB = ("dp_0", "dp_1", "dp_2", "vocab_0", "vocab_1")


def whole_of(shard, axes, dim):
    filled = shard
    for number in range(len(axes) - 1, -1, -1):
        filled = lax.all_gather(filled, axes[number], axis=dim, tiled=True)
    return filled


def all_in_one(shard, axis):
    leaves = jax.tree.leaves(shard)
    sequence = sorted(range(len(leaves)), key=lambda k: -leaves[k].size)
    width = (1, *leaves[sequence[0]].shape)[-1]
    lines = [
        jnp.pad(leaves[k].reshape(-1), (0, -leaves[k].size % width)).reshape(-1, width)
        for k in sequence
    ]
    both, at, found = (lax.all_gather(jnp.concatenate(lines), axis), 0, {})
    for k, line in zip(sequence, lines):
        share = both[:, at : at + len(line)].reshape(len(both), -1)
        found[k] = share[:, : leaves[k].size].reshape(-1, *leaves[k].shape)
        at += len(line)
    numbers = iter(range(len(leaves)))
    return jax.tree.map(lambda _: found[next(numbers)], shard)


def combined_all(shard, axis, combine):
    everything = all_in_one(shard, axis)
    first = jax.tree.map(lambda part: part[0], everything)

    def turn(k, so_far):
        return combine(so_far, jax.tree.map(lambda part: part[k], everything))

    return lax.fori_loop(1, lax.axis_size(axis), turn, first)


def one_axis_at_a_time(shard, axes):
    return functools.reduce(lax.psum, axes, shard)


def merge_rows(earlier, later):
    maxima = jnp.maximum(earlier[0], later[0])
    totals = earlier[1] * jnp.exp(earlier[0] - maxima) + later[1] * jnp.exp(later[0] - maxima)
    return (maxima, totals, earlier[2] + later[2])


def local(hidden, targets, lengths, head):
    whole_head, all_lengths = (
        lax.all_gather(head, DP, axis=0, tiled=True),
        lax.all_gather(lengths, DP, axis=0, tiled=True),
    )
    clip_rows, clip_targets = (whole_of(hidden, VOCAB, 0), whole_of(targets, VOCAB, 0))
    level_count = whole_head.shape[1]
    home_rows = hidden.shape[0]
    logits = jnp.dot(clip_rows, whole_head, preferred_element_type=jnp.float32)
    local_levels = clip_targets - lax.axis_index(VOCAB) * level_count
    level_grid = jnp.arange(level_count, dtype=jnp.int32)
    is_target = local_levels[:, None] == level_grid[None, :]
    target_logit = jnp.sum(jnp.where(is_target, logits, 0.0), axis=1)
    maxima = jnp.max(logits, axis=1)
    totals = jnp.sum(jnp.exp(logits - maxima[:, None]), axis=1)
    maxima, totals, target_logit = combined_all((maxima, totals, target_logit), VOCAB, merge_rows)
    log_total = maxima + jnp.log(totals)
    total_count = jnp.sum(all_lengths).astype(jnp.float32)
    clip_index = jnp.arange(all_lengths.shape[0], dtype=jnp.int32)
    clip_length = jnp.sum(jnp.where(clip_index == lax.axis_index(DP), all_lengths, 0))
    positions = jnp.arange(clip_rows.shape[0], dtype=jnp.int32)
    valid_rows = (positions < clip_length).astype(jnp.float32)
    row_loss = valid_rows * (log_total - target_logit)
    home_loss = jnp.sum(
        lax.dynamic_slice_in_dim(row_loss, lax.axis_index(VOCAB) * home_rows, home_rows, 0)
    )
    loss = one_axis_at_a_time(home_loss, DP_VOCAB) / total_count
    weights = (valid_rows / total_count)[:, None]
    grad_logits = (
        weights * (jnp.exp(logits - log_total[:, None]) - is_target.astype(jnp.float32))
    ).astype(jnp.bfloat16)
    grad_home = lax.psum_scatter(
        lax.dot_general(
            grad_logits, whole_head, (((1,), (1,)), ((), ())), preferred_element_type=jnp.float32
        ),
        VOCAB,
        scatter_dimension=0,
        tiled=True,
    )
    return (grad_home.astype(jnp.bfloat16), loss)


def solution(mesh):
    torus = Mesh(
        mesh.devices.reshape(2, 8, 2, 4, 2), ("dp_0", "dp_1", "dp_2", "vocab_0", "vocab_1")
    )
    return jax.shard_map(
        local,
        mesh=torus,
        in_specs=(P(DP_VOCAB, None), P(DP_VOCAB), P(DP), P(DP, VOCAB)),
        out_specs=(P(DP_VOCAB, None), P()),
        check_vma=False,
    )
```

profile of v0, /device:TPU:1, one launch (start us, length us, event | category | flops | bytes accessed | tf_op | source)
XLA Modules:
  0.0 381.4 jit_solution(14241844789752872180)
XLA Ops:
  7.2 0.0 all-gather.6.cloned.1.call-start
  7.2 13.1 %all_gather.25 = bf16[128,3072]{1,0:T(8,128)(2,1)} all-gather(bf16[64,3072]{1,0:T(8,128)(2,1)} %param.6), channel_id=1, replica_groups=mesh['dp_0'=2,'dp_1'=8,'dp_2'=2,'vocab_0'=4,'vocab_1'=2] {'vocab_1'}, dimensions={0}, use_global_device_ids=true | all-gather | bytes 1179648 | tf_op jit(solution)/shard_map/all_gather | solution.py:16
  20.4 0.0 all-gather.6.cloned.1.call-update
  20.4 0.0 all-gather.8.cloned.1.call-start
  20.4 0.7 all-gather.8.cloned.1.call-update
  21.1 0.0 reduce-scatter.2.cloned.1.call-start
  21.8 1.3 dynamic-slice.1
  23.1 1.2 dynamic-slice
  24.3 0.7 dynamic-update-slice
  25.0 18.6 %all-reduce = s32[32]{0:T(128)S(1)} all-reduce(s32[32]{0:T(128)S(1)} %dynamic-update-slice), channel_id=1, replica_groups=mesh['dp_0'=2,'dp_1'=8,'dp_2'=2,'vocab_0'=4,'vocab_1'=2] {'dp_0','dp_1',..., use_global_device_ids=true, to_apply=%add | all-reduce | flops 32 | bytes 256
  43.6 0.6 fusion.5
  45.6 0.9 dynamic-update-slice.1
  46.4 3.5 all-reduce.1
  49.9 8.8 %all-gather.1 = s32[4,1,128]{2,1,0:T(1,128)S(1)} all-gather(s32[1,1,128]{2,1,0:T(1,128)S(1)} %bitcast.43), channel_id=1, replica_groups=mesh['dp_0'=2,'dp_1'=8,'dp_2'=2,'vocab_0'=4,'vocab_1'=2] {'vocab_0'}, dimensions={0}, use_global_device_ids=true | all-gather | bytes 2560 | tf_op jit(solution)/shard_map/all_gather | solution.py:16
  58.7 0.5 fusion.4
  59.3 6.9 %all-gather.6.cloned.1.call-done = bf16[512,3072]{1,0:T(8,128)(2,1)} async-done(((bf16[128,3072]{1,0:T(8,128)(2,1)}), bf16[512,3072]{1,0:T(8,128)(2,1)}) %all-gather.6.cloned.1.call-update) | async-done | bytes 3145744 | tf_op jit(solution)/shard_map/all_gather | solution.py:16
  66.1 120.7 %all-gather.8.cloned.1.call-done = bf16[3072,2048]{1,0:T(8,128)(2,1)} async-done(((bf16[96,2048]{1,0:T(8,128)(2,1)}), bf16[3072,2048]{1,0:T(8,128)(2,1)}) %all-gather.8.cloned.1.call-update) | async-done | bytes 12582928 | tf_op jit(solution)/shard_map/all_gather | solution.py:59
  186.8 10.7 %fusion.8 = (f32[512]{0:T(512)S(1)}, f32[512,2048]{1,0:T(8,128)S(1)}) fusion(bf16[512,3072]{1,0:T(8,128)(2,1)} %all-gather.6.cloned.1.call-done, bf16[3072,2048]{1,0:T(8,128)(2,1)} %all-gather.8.cloned.1.call-done), kind=kOutput, calls=%fused_computation.26 | convolution fusion | flops 6443499008 | bytes 19924992 | tf_op jit(solution)/shard_map/dot_general | solution.py:65
  197.5 0.0 copy-start
  197.5 2.0 copy-done
  199.6 1.1 exponential_reduce_fusion
  200.7 21.8 %all-gather.2 = f32[8,3,512]{2,1,0:T(4,128)S(1)} all-gather(f32[1,3,512]{2,1,0:T(4,128)S(1)} %maximum_bitcast_fusion), channel_id=2, replica_groups=mesh['dp_0'=2,'dp_1'=8,'dp_2'=2,'vocab_0'=4,'vocab_1'=2] {'vocab_0','voc..., dimensions={0}, use_global_device_ids=true | all-gather | bytes 55296 | tf_op jit(solution)/shard_map/all_gather | solution.py:28
  222.6 0.6 while.19
  223.2 0.6 subtract_select_fusion
  223.8 13.1 %fusion = f32[512,3072]{1,0:T(8,128)} fusion(bf16[3072,2048]{1,0:T(8,128)(2,1)} %all-gather.8.cloned.1.call-done, f32[512,2048]{1,0:T(8,128)} %copy-done, f32[512]{0:T(512)S(1)} %get-tuple-element.204, s32[512]{0:T(512)S(1)} %bitcast.42, f32[512]{0:T(512)S(1)} %fusion.4), kind=kOutput, calls=%fused_computation.8 | convolution fusion | flops 6448742400 | bytes 23074816 | tf_op jit(solution)/shard_map/dot_general | solution.py:89
  236.9 0.0 reduce-scatter.2.cloned.1.call-update
  236.9 0.7 dynamic-slice_reduce_fusion
  237.6 5.9 %psum.35 = f32[]{:T(128)} all-reduce(f32[]{:T(128)} %dynamic-slice_reduce_fusion), channel_id=1, replica_groups=mesh['dp_0'=2,'dp_1'=8,'dp_2'=2,'vocab_0'=4,'vocab_1'=2] {'dp_0'}, use_global_device_ids=true, to_apply=%region_9.10 | all-reduce | flops 1 | bytes 8 | tf_op jit(solution)/shard_map/psum | solution.py:48
  243.5 13.3 %psum.36 = f32[]{:T(128)} all-reduce(f32[]{:T(128)} %psum.35), channel_id=1, replica_groups=mesh['dp_0'=2,'dp_1'=8,'dp_2'=2,'vocab_0'=4,'vocab_1'=2] {'dp_1'}, use_global_device_ids=true, to_apply=%region_10.11 | all-reduce | flops 1 | bytes 8 | tf_op jit(solution)/shard_map/psum | solution.py:48
  256.8 13.9 %psum.37 = f32[]{:T(128)} all-reduce(f32[]{:T(128)} %psum.36), channel_id=1, replica_groups=mesh['dp_0'=2,'dp_1'=8,'dp_2'=2,'vocab_0'=4,'vocab_1'=2] {'dp_2'}, use_global_device_ids=true, to_apply=%region_11.12 | all-reduce | flops 1 | bytes 8 | tf_op jit(solution)/shard_map/psum | solution.py:48
  270.7 6.9 %psum.38 = f32[]{:T(128)} all-reduce(f32[]{:T(128)} %psum.37), channel_id=1, replica_groups=mesh['dp_0'=2,'dp_1'=8,'dp_2'=2,'vocab_0'=4,'vocab_1'=2] {'vocab_0'}, use_global_device_ids=true, to_apply=%region_12.13 | all-reduce | flops 1 | bytes 8 | tf_op jit(solution)/shard_map/psum | solution.py:48
  277.5 6.2 %psum.39 = f32[]{:T(128)} all-reduce(f32[]{:T(128)} %psum.38), channel_id=1, replica_groups=mesh['dp_0'=2,'dp_1'=8,'dp_2'=2,'vocab_0'=4,'vocab_1'=2] {'vocab_1'}, use_global_device_ids=true, to_apply=%region_13.14 | all-reduce | flops 1 | bytes 8 | tf_op jit(solution)/shard_map/psum | solution.py:48
  284.4 87.4 %reduce-scatter.2.cloned.1.call-done = f32[64,3072]{1,0:T(8,128)} async-done(((f32[512,3072]{1,0:T(8,128)}), f32[64,3072]{1,0:T(8,128)}) %reduce-scatter.2.cloned.1.call-update) | async-done | bytes 786448 | tf_op jit(solution)/shard_map/reduce_scatter | solution.py:88
  371.8 1.9 convert_element_type.17
  (36 shorter events, 0.4 us)
Async XLA Ops:
  7.2 59.0 %all-gather.6.cloned.1.call-start = ((), (), s32[]{:S(2)}) async-start(), calls=%async_computation.1 | async-start | bytes 3932160 | tf_op jit(solution)/shard_map/all_gather | solution.py:16
  20.4 166.4 %all-gather.8.cloned.1.call-start = ((), (), s32[]{:S(2)}) async-start(), calls=%async_computation.2 | async-start | bytes 12976128 | tf_op jit(solution)/shard_map/all_gather | solution.py:59
  21.1 350.7 %reduce-scatter.2.cloned.1.call-start = ((), (), s32[]{:S(2)}) async-start(), calls=%async_computation.3 | async-start | bytes 7077888 | tf_op jit(solution)/shard_map/reduce_scatter | solution.py:88
  197.5 2.0 copy-start
Sparse Core Ops, SparseCore 0:
  20.5 45.5 all-gather.5
  68.9 117.8 all-gather.7
  237.0 134.7 reduce-scatter.1
where the time goes:
time: 382 us; the launch traced here: 381 us
  waiting for transfers between devices  216 us (57%)
  blocking collectives  112 us (29%)
  matrix products  23.8 us (6%)
  between operations  17.6 us (5%)
  local copies, waits for them, and re-layouts  6.23 us (2%)
  other arithmetic  5.71 us (1%)
    all_gather x1, waiting for transfers between devices, local(): lax.all_gather(head, DP, axis=0, tiled=True)  121 us
    reduce_scatter x1, waiting for transfers between devices, local(): lax.psum_scatter(lax.dot_general(grad_logits, whole_head, (((1,), (1,)),...  87.4 us
    psum x5, blocking collectives, one_axis_at_a_time(): return functools.reduce(lax.psum, axes, shard)  46.2 us
    unnamed x2, blocking collectives  22.1 us
    all_gather x2, blocking collectives, whole_of(): filled = lax.all_gather(filled, axes[number], axis=dim, tiled=True)  21.9 us
    all_gather x1, blocking collectives, all_in_one(): both, at, found = (lax.all_gather(jnp.concatenate(lines), axis), 0, {})  21.8 us
    dot_general x1, matrix products, local(): lax.dot_general(grad_logits, whole_head, (((1,), (1,)), ((), ())), prefer...  13.1 us
    dot_general x1, matrix products, local(): logits = jnp.dot(clip_rows, whole_head, preferred_element_type=jnp.float32)  10.7 us
  transfers between devices with their start and end apart: 3, of which 3 were waited for; matrix products, arithmetic and copies ran while one was open for 2% of the time, Pallas kernels for 0%

commit v1 on v0

--- a/solution.py
+++ b/solution.py
@@ -56,7 +56,7 @@
 
 def local(hidden, targets, lengths, head):
     whole_head, all_lengths = (
-        lax.all_gather(head, DP, axis=0, tiled=True),
+        jnp.concatenate(lax.all_to_all(jnp.stack([head] * lax.axis_size(DP)), DP, 0, 0), axis=0),
         lax.all_gather(lengths, DP, axis=0, tiled=True),
     )
     clip_rows, clip_targets = (whole_of(hidden, VOCAB, 0), whole_of(targets, VOCAB, 0))

time: 382 us -> 526 us (1.38)
  blocking collectives: 112 us -> 366 us
  waiting for transfers between devices: 216 us -> 86.4 us
  starting transfers between devices: 0.12 us -> 13 us
  local copies, waits for them, and re-layouts: 6.23 us -> 11.6 us
    unnamed x2, blocking collectives: 22.1 us -> 246 us
    all_gather x1 -> x0, waiting for transfers between devices: 121 us -> none  [local(): lax.all_gather(head, DP, axis=0, tiled=True)]
    all_gather x2, blocking collectives: 21.9 us -> 49.1 us  [whole_of(): filled = lax.all_gather(filled, axes[number], axis=dim, tiled=True)]
    all_to_all x0 -> x1, starting transfers between devices: none -> 12.9 us  [local(): lax.all_to_all(jnp.stack([head] * lax.axis_size(DP)), DP, 0, 0)]
    another operation x0 -> x1, local copies, waits for them, and re-layouts: none -> 7.07 us  [local(): jnp.stack([head] * lax.axis_size(DP))]
    all_gather x1, waiting for transfers between devices: 6.85 us -> 0.02 us  [whole_of(): filled = lax.all_gather(filled, axes[number], axis=dim, tiled=True)]
  transfers between devices with their start and end apart: 3 -> 3, of which waited for: 3 -> 1; matrix products, arithmetic and copies ran while one was open for 2% -> 1% of each run, Pallas kernels for 0% -> 0%
where the time goes in v1:
time: 526 us; the launch traced here: 525 us
  blocking collectives  366 us (70%)
  waiting for transfers between devices  86.4 us (16%)
  matrix products  23.8 us (5%)
  between operations  18 us (3%)
  starting transfers between devices  13 us (2%)
  local copies, waits for them, and re-layouts  11.6 us (2%)
  other arithmetic  6.01 us (1%)
    unnamed x2, blocking collectives  246 us
    reduce_scatter x1, waiting for transfers between devices, local(): lax.psum_scatter(lax.dot_general(grad_logits, whole_head, (((1,), (1,)),...  86.4 us
    psum x5, blocking collectives, one_axis_at_a_time(): return functools.reduce(lax.psum, axes, shard)  49.8 us
    all_gather x2, blocking collectives, whole_of(): filled = lax.all_gather(filled, axes[number], axis=dim, tiled=True)  49.1 us
    all_gather x1, blocking collectives, all_in_one(): both, at, found = (lax.all_gather(jnp.concatenate(lines), axis), 0, {})  21.9 us
    dot_general x1, matrix products, local(): lax.dot_general(grad_logits, whole_head, (((1,), (1,)), ((), ())), prefer...  13.1 us
    all_to_all x1, starting transfers between devices, local(): lax.all_to_all(jnp.stack([head] * lax.axis_size(DP)), DP, 0, 0)  12.9 us
    dot_general x1, matrix products, local(): logits = jnp.dot(clip_rows, whole_head, preferred_element_type=jnp.float32)  10.7 us
  transfers between devices with their start and end apart: 3, of which 1 were waited for; matrix products, arithmetic and copies ran while one was open for 1% of the time, Pallas kernels for 0%

profile of v1, /device:TPU:1, one launch (start us, length us, event | category | flops | bytes accessed | tf_op | source)
XLA Modules:
  0.0 525.4 jit_solution(14798573958116979966)
XLA Ops:
  7.2 7.1 %stack.2 = bf16[32,96,2048]{2,1,0:T(8,128)(2,1)} broadcast(bf16[96,2048]{1,0:T(8,128)(2,1)} %param.9), dimensions={1,2} | broadcast | bytes 12976128 | tf_op jit(solution)/shard_map/stack | solution.py:59
  14.2 0.0 copy-start.1
  14.2 0.0 copy-start.4
  14.2 0.0 copy-start.3
  14.2 0.0 copy-start.2
  14.2 12.9 %all-to-all-start = ((bf16[32,96,2048]{2,1,0:T(8,128)(2,1)}), bf16[32,96,2048]{2,1,0:T(8,128)(2,1)}, u32[]{:S(2)}, u32[]{:S(2)}) async-start(bf16[32,96,2048]{2,1,0:T(8,128)(2,1)} %stack.2), calls=%async_computation | async-start | bytes 25165824 | tf_op jit(solution)/shard_map/all_to_all | solution.py:59
  27.2 0.0 all-gather.5.cloned.1.call-start
  27.2 0.0 copy-done.1
  27.2 41.4 %all_gather.22 = bf16[128,3072]{1,0:T(8,128)(2,1)} all-gather(bf16[64,3072]{1,0:T(8,128)(2,1)S(1)} %copy-done.1), channel_id=1, replica_groups=mesh['dp_0'=2,'dp_1'=8,'dp_2'=2,'vocab_0'=4,'vocab_1'=2] {'vocab_1'}, dimensions={0}, use_global_device_ids=true | all-gather | bytes 1179648 | tf_op jit(solution)/shard_map/all_gather | solution.py:16
  68.6 0.0 all-gather.5.cloned.1.call-update
  68.6 0.0 reduce-scatter.2.cloned.1.call-start
  69.3 0.0 copy-done.4
  69.4 0.6 dynamic-slice.1
  69.9 0.0 copy-done.3
  69.9 0.6 dynamic-slice
  70.6 0.8 dynamic-update-slice
  71.4 242.5 %all-reduce = s32[32]{0:T(128)S(1)} all-reduce(s32[32]{0:T(128)S(1)} %dynamic-update-slice), channel_id=1, replica_groups=mesh['dp_0'=2,'dp_1'=8,'dp_2'=2,'vocab_0'=4,'vocab_1'=2] {'dp_0','dp_1',..., use_global_device_ids=true, to_apply=%add | all-reduce | flops 32 | bytes 256
  313.9 0.7 fusion.5
  315.9 0.0 copy-done.2
  315.9 0.2 dynamic-update-slice.1
  316.2 3.1 all-reduce.1
  319.3 7.7 %all-gather.1 = s32[4,1,128]{2,1,0:T(1,128)S(1)} all-gather(s32[1,1,128]{2,1,0:T(1,128)S(1)} %bitcast.44), channel_id=1, replica_groups=mesh['dp_0'=2,'dp_1'=8,'dp_2'=2,'vocab_0'=4,'vocab_1'=2] {'vocab_0'}, dimensions={0}, use_global_device_ids=true | all-gather | bytes 2560 | tf_op jit(solution)/shard_map/all_gather | solution.py:16
  327.0 0.7 fusion.4
  327.7 0.0 all-gather.5.cloned.1.call-done
  327.7 0.0 all-to-all-done
  327.7 10.7 %fusion.8 = (f32[512]{0:T(512)S(1)}, f32[512,2048]{1,0:T(8,128)S(1)}) fusion(bf16[512,3072]{1,0:T(8,128)(2,1)} %all-gather.5.cloned.1.call-done, bf16[3072,2048]{1,0:T(8,128)(2,1)} %bitcast.4), kind=kOutput, calls=%fused_computation.26 | convolution fusion | flops 6443499008 | bytes 19924992 | tf_op jit(solution)/shard_map/dot_general | solution.py:65
  338.4 0.0 copy-start
  338.4 2.0 copy-done
  340.5 1.1 exponential_reduce_fusion
  341.6 21.9 %all-gather.2 = f32[8,3,512]{2,1,0:T(4,128)S(1)} all-gather(f32[1,3,512]{2,1,0:T(4,128)S(1)} %maximum_bitcast_fusion), channel_id=2, replica_groups=mesh['dp_0'=2,'dp_1'=8,'dp_2'=2,'vocab_0'=4,'vocab_1'=2] {'vocab_0','voc..., dimensions={0}, use_global_device_ids=true | all-gather | bytes 55296 | tf_op jit(solution)/shard_map/all_gather | solution.py:28
  363.6 0.6 while.19
  364.2 0.7 subtract_select_fusion
  364.9 13.1 %fusion = f32[512,3072]{1,0:T(8,128)} fusion(bf16[3072,2048]{1,0:T(8,128)(2,1)} %bitcast.4, f32[512,2048]{1,0:T(8,128)} %copy-done, f32[512]{0:T(512)S(1)} %get-tuple-element.204, s32[512]{0:T(512)S(1)} %bitcast.43, f32[512]{0:T(512)S(1)} %fusion.4), kind=kOutput, calls=%fused_computation.8 | convolution fusion | flops 6448742400 | bytes 23074816 | tf_op jit(solution)/shard_map/dot_general | solution.py:89
  377.9 0.0 reduce-scatter.2.cloned.1.call-update
  378.0 0.7 dynamic-slice_reduce_fusion
  378.6 5.9 %psum.35 = f32[]{:T(128)} all-reduce(f32[]{:T(128)} %dynamic-slice_reduce_fusion), channel_id=1, replica_groups=mesh['dp_0'=2,'dp_1'=8,'dp_2'=2,'vocab_0'=4,'vocab_1'=2] {'dp_0'}, use_global_device_ids=true, to_apply=%region_9.10 | all-reduce | flops 1 | bytes 8 | tf_op jit(solution)/shard_map/psum | solution.py:48
  384.5 11.3 %psum.36 = f32[]{:T(128)} all-reduce(f32[]{:T(128)} %psum.35), channel_id=1, replica_groups=mesh['dp_0'=2,'dp_1'=8,'dp_2'=2,'vocab_0'=4,'vocab_1'=2] {'dp_1'}, use_global_device_ids=true, to_apply=%region_10.11 | all-reduce | flops 1 | bytes 8 | tf_op jit(solution)/shard_map/psum | solution.py:48
  395.8 20.1 %psum.37 = f32[]{:T(128)} all-reduce(f32[]{:T(128)} %psum.36), channel_id=1, replica_groups=mesh['dp_0'=2,'dp_1'=8,'dp_2'=2,'vocab_0'=4,'vocab_1'=2] {'dp_2'}, use_global_device_ids=true, to_apply=%region_11.12 | all-reduce | flops 1 | bytes 8 | tf_op jit(solution)/shard_map/psum | solution.py:48
  416.0 7.5 %psum.38 = f32[]{:T(128)} all-reduce(f32[]{:T(128)} %psum.37), channel_id=1, replica_groups=mesh['dp_0'=2,'dp_1'=8,'dp_2'=2,'vocab_0'=4,'vocab_1'=2] {'vocab_0'}, use_global_device_ids=true, to_apply=%region_12.13 | all-reduce | flops 1 | bytes 8 | tf_op jit(solution)/shard_map/psum | solution.py:48
  423.5 5.0 psum.39
  429.1 86.4 %reduce-scatter.2.cloned.1.call-done = f32[64,3072]{1,0:T(8,128)} async-done(((f32[512,3072]{1,0:T(8,128)}), f32[64,3072]{1,0:T(8,128)}) %reduce-scatter.2.cloned.1.call-update) | async-done | bytes 786448 | tf_op jit(solution)/shard_map/reduce_scatter | solution.py:88
  515.5 1.9 convert_element_type.17
  (36 shorter events, 0.4 us)
Async XLA Ops:
  14.2 13.0 %copy-start.1 = (bf16[64,3072]{1,0:T(8,128)(2,1)S(1)}, bf16[64,3072]{1,0:T(8,128)(2,1)}, u32[]{:S(2)}) copy-start(bf16[64,3072]{1,0:T(8,128)(2,1)} %param.6) | copy-start | bytes 1179652
  14.2 55.1 %copy-start.4 = (u32[256]{0:T(256)S(1)}, u32[256]{0:T(256)}, u32[]{:S(2)}) copy-start(u32[256]{0:T(256)} %constant.85) | copy-start | bytes 3076
  14.2 55.7 %copy-start.3 = (u32[256]{0:T(256)S(1)}, u32[256]{0:T(256)}, u32[]{:S(2)}) copy-start(u32[256]{0:T(256)} %constant.80) | copy-start | bytes 3076
  14.2 301.7 %copy-start.2 = (s32[64]{0:T(128)S(1)}, s32[64]{0:T(128)}, u32[]{:S(2)}) copy-start(s32[64]{0:T(128)} %param.7) | copy-start | bytes 772
  14.2 313.4 %all-to-all-start = ((bf16[32,96,2048]{2,1,0:T(8,128)(2,1)}), bf16[32,96,2048]{2,1,0:T(8,128)(2,1)}, u32[]{:S(2)}, u32[]{:S(2)}) async-start(bf16[32,96,2048]{2,1,0:T(8,128)(2,1)} %stack.2), calls=%async_computation | async-start | bytes 25165824 | tf_op jit(solution)/shard_map/all_to_all | solution.py:59
  27.2 300.5 %all-gather.5.cloned.1.call-start = ((), (), s32[]{:S(2)}) async-start(), calls=%async_computation.2 | async-start | bytes 3932160 | tf_op jit(solution)/shard_map/all_gather | solution.py:16
  68.6 446.9 %reduce-scatter.2.cloned.1.call-start = ((), (), s32[]{:S(2)}) async-start(), calls=%async_computation.3 | async-start | bytes 7077888 | tf_op jit(solution)/shard_map/reduce_scatter | solution.py:88
  338.4 2.0 copy-start
Sparse Core Ops, SparseCore 0:
  68.8 45.8 all-gather.4
  378.1 137.3 reduce-scatter.1
